TPU v7x, 32 devices: a whole 2x2x4 slice. The times are simulated.
32 devices in a mesh: tm: 8 (over z, x), lev: 4 (over y, core).
Axes of the slice: x: 2, y: 2, z: 4, core: 2. Of those that a mesh axis runs over, the one named last changes fastest.
Arguments:
- increment: float32 [8, 3, 8, 256, 512], P('tm', None, 'lev'), may hold values from -6 to 6
- multiplier: float32 [8, 3, 8, 256, 512], P('tm', None, 'lev'), may hold values from -6 to 6
- error_var: float32 [8, 3, 8, 256, 512], P('tm', None, 'lev'), may hold values from 0.1 to 1
- obs_cell: int32 [8, 8, 512], P('tm', 'lev'), may hold values from 0 to 131071
- obs_dual: float32 [8, 8, 512], P('tm', 'lev'), may hold values from -6 to 6
- obs_var: float32 [8, 8, 512], P('tm', 'lev'), may hold values from 0.5 to 2
- level_gain: float32 [8], P('lev'), may hold values from 0.5 to 1.5
- mean_depth: float32 [8], P('lev'), may hold values from 0.5 to 2
- chain_decay: float32 [8, 3, 8], P('tm', None, 'lev'), may hold values from 0 to 1
Outputs:
- dual_product: float32 [8, 3, 8, 256, 512], P('tm', None, 'lev')
- obs_product: float32 [8, 8, 512], P('tm', 'lev')
- state_block_product: float32 [8, 3, 8, 256, 512], P('tm', None, 'lev')
- chain_solution: float32 [8, 3, 8, 256, 512], P('tm', None, 'lev')
All inputs are finite; a program needn't handle non-finite values.
Results may differ from a plain program's by a relative error of at most 0.0001.
Values sent between devices are 32-bit elements; how exact they have to be, the bound alone decides.
A program may use at most 320 MiB of HBM per device.

v0:
```python
import jax
import jax.numpy as jnp
from jax import lax
from jax.sharding import PartitionSpec as P

STEPS = 2


TIME_STEP = 0.25
ROTATION_PARAM = 0.5
COUPLING = 0.25


def shifted(block, axis, distance):
    devices = range(lax.axis_size(axis))
    route = [(i - distance, i) for i in devices if i - distance in devices]
    return lax.ppermute(block, axis, route)


def prefix_2(part, axis, combine, identity):
    place = lax.axis_index(axis)
    gathered = jax.tree.map(lambda a: lax.all_gather(a, axis), part)
    state = jax.tree.map(lambda a, e: jnp.zeros_like(a) + jnp.asarray(e, a.dtype), part, identity)

    def one(lap, state):
        return combine(
            state, jax.tree.map(lambda a: lax.dynamic_index_in_dim(a, lap, 0, False), gathered)
        )

    return lax.fori_loop(0, place, one, state)


def dynamics_advance(state, column, level_gain, mean_depth):
    h, u, v = (state[0], state[1], state[2])
    p = level_gain[:, None, None] * h + COUPLING * column[None]
    gradient_eastward = jnp.concatenate([p[:, 1:, :], jnp.zeros_like(p[:, :1, :])], axis=1) - p
    grad_y = jnp.concatenate([p[:, :, 1:], jnp.zeros_like(p[:, :, :1])], axis=2) - p
    u_new = u + TIME_STEP * (ROTATION_PARAM * v - gradient_eastward)
    v_new = v - TIME_STEP * (ROTATION_PARAM * u + grad_y)
    back_x = u_new - jnp.concatenate([jnp.zeros_like(u_new[:, :1, :]), u_new[:, :-1, :]], axis=1)
    back_y = v_new - jnp.concatenate([jnp.zeros_like(v_new[:, :, :1]), v_new[:, :, :-1]], axis=2)
    h_new = h - TIME_STEP * mean_depth[:, None, None] * (back_x + back_y)
    return jnp.stack([h_new, u_new, v_new])


def combine(earlier, later):
    return (later[0] * earlier[0], later[0][:, :, None, None] * earlier[1] + later[1])


def shards(
    increment,
    multiplier,
    error_var,
    obs_cell,
    obs_dual,
    obs_var,
    level_gain,
    mean_depth,
    chain_decay,
):
    state_dx = increment[0]
    dual = multiplier[0]
    zero_column = jnp.zeros_like(state_dx[0, 0])

    def transpose_step(state):

        def local_map(state_in, column):
            return dynamics_advance(state_in, column, level_gain, mean_depth)

        return jax.vjp(local_map, jnp.zeros_like(state), zero_column)[1](state)

    source = shifted(dual, "tm", -1)
    tangent = state_dx
    adjoint_state = source
    for step in range(STEPS):
        column = lax.psum(jnp.sum(tangent[0], axis=0), "lev")
        tangent = dynamics_advance(tangent, column, level_gain, mean_depth)
    for step in range(STEPS):
        local_part, bar_column = transpose_step(adjoint_state)
        total = lax.psum(bar_column, "lev")
        adjoint_state = local_part.at[0].add(total[None])
    arrived = shifted(tangent, "tm", 1)
    dual_product = error_var[0] * dual + state_dx - arrived
    levels_here = state_dx.shape[1]
    flat_h = state_dx[0].reshape(levels_here, -1)
    picked = jnp.take_along_axis(flat_h, obs_cell[0], axis=1)
    obs_product = obs_var[0] * obs_dual[0] + picked

    def spread(cells, values):
        return jnp.zeros((flat_h.shape[1],), jnp.float32).at[cells].add(values)

    added = jax.vmap(spread)(obs_cell[0], obs_dual[0]).reshape(state_dx[0].shape)
    state_block_product = (dual - adjoint_state).at[0].add(added)
    scale_multiplier = chain_decay[0]
    prefix = prefix_2(
        (scale_multiplier, dual_product),
        "tm",
        combine,
        (jnp.ones_like(scale_multiplier), jnp.zeros_like(dual_product)),
    )
    chain_solution = scale_multiplier[:, :, None, None] * prefix[1] + dual_product
    return (dual_product[None], obs_product[None], state_block_product[None], chain_solution[None])


def solution(mesh):
    return jax.shard_map(
        shards,
        mesh=mesh,
        in_specs=(
            P("tm", None, "lev", None, None),
            P("tm", None, "lev", None, None),
            P("tm", None, "lev", None, None),
            P("tm", "lev", None),
            P("tm", "lev", None),
            P("tm", "lev", None),
            P("lev"),
            P("lev"),
            P("tm", None, "lev"),
        ),
        out_specs=(
            P("tm", None, "lev", None, None),
            P("tm", "lev", None),
            P("tm", None, "lev", None, None),
            P("tm", None, "lev", None, None),
        ),
        check_vma=False,
    )
```

profile of v0, /device:TPU:31, one launch (start us, length us, event | category | flops | bytes accessed | tf_op | source)
XLA Modules:
  0.0 776.2 jit_solution(5688045770264279408)
XLA Ops:
  7.2 2.4 collective-permute-start.1
  9.6 0.7 broadcast_multiply_fusion.6
  10.2 3.3 slice_bitcast_fusion.5
  13.5 62.9 %collective-permute-done.1 = f32[3,2,256,512]{3,2,1,0:T(8,128)S(1)} collective-permute-done((f32[3,2,256,512]{3,2,1,0:T(8,128)}, f32[3,2,256,512]{3,2,1,0:T(8,128)S(1)}, u32[]{:S(2)}, u32[]{:S(2)}) %collective-permute-start.1) | collective-permute-done | bytes 3145760 | tf_op jit(solution)/shard_map/ppermute | solution.py:17
  76.5 0.2 fusion.19
  76.7 0.3 split.32
  77.0 0.1 split.33
  77.2 1.7 add_bitcast_fusion.6
  78.9 0.2 negate_multiply_fusion.3
  79.2 0.1 slice_negate_fusion.1
  79.3 0.3 copy-done.19
  79.6 2.1 add_bitcast_fusion.4
  81.7 0.1 reduce_sum.37
  81.8 0.8 broadcast_multiply_fusion.3
  82.7 2.2 pad_add_fusion.1
  84.9 37.1 %all-reduce.29.cloned.1.call-done = (f32[256,512]{1,0:T(8,128)}, f32[256,512]{1,0:T(8,128)}) async-done(((f32[256,512]{1,0:T(8,128)}, f32[256,512]{1,0:T(8,128)}), (f32[256,512]{1,0:T(8,128)}, f32[256,512]{1,0:T(8,128)})) %all-reduce.29.cloned.1.call-update) | async-done | bytes 1048592 | tf_op jit(solution)/shard_map/psum | solution.py:76
  122.0 1.5 fusion.20
  123.5 0.3 split.36
  123.8 0.1 split.37
  124.0 1.7 add_bitcast_fusion.3
  126.0 0.7 copy-done.16
  126.7 3.7 add_bitcast_fusion.1
  130.5 1.1 slice.135
  131.6 0.2 copy-done.2
  131.8 1.3 slice.137
  133.1 2.2 reduce_sum.41
  135.3 1.9 broadcast_multiply_fusion.2
  137.2 2.5 fusion.15
  139.7 2.4 fusion.28
  142.2 36.9 %all-reduce.27.cloned.1.call-done = (f32[256,512]{1,0:T(8,128)}, f32[256,512]{1,0:T(8,128)}) async-done(((f32[256,512]{1,0:T(8,128)}, f32[256,512]{1,0:T(8,128)}), (f32[256,512]{1,0:T(8,128)}, f32[256,512]{1,0:T(8,128)})) %all-reduce.27.cloned.1.call-update) | async-done | bytes 1048592 | tf_op jit(solution)/shard_map/psum | solution.py:76
  179.2 1.1 broadcast_multiply_fusion.4
  180.3 1.6 multiply_add_fusion.1
  181.9 0.1 slice.139
  182.0 0.3 slice.141
  182.4 0.8 multiply_add_fusion
  183.2 0.5 subtract_bitcast_fusion
  183.7 0.3 pad_maximum_fusion
  184.0 1.6 collective-permute-start
  185.7 0.3 pad_add_fusion
  186.0 0.7 copy-done.15
  186.7 0.2 fusion.3
  186.9 68.0 %collective-permute-done = f32[3,2,256,512]{3,2,1,0:T(8,128)} collective-permute-done((f32[3,2,256,512]{3,2,1,0:T(8,128)S(1)}, f32[3,2,256,512]{3,2,1,0:T(8,128)}, u32[]{:S(2)}, u32[]{:S(2)}) %collective-permute-start) | collective-permute-done | bytes 3145760 | tf_op jit(solution)/shard_map/ppermute | solution.py:17
  255.0 7.5 bitcast_subtract_fusion.2
  262.5 1.2 copy-done.10
  263.7 0.8 copy.19
  264.6 9.1 %gather_fusion = f32[1024]{0:T(1024)S(1)} fusion(f32[2,131072]{1,0:T(2,128)S(1)} %bitcast.150, s32[1024]{0:T(1024)S(1)} %bitcast.148), kind=kCustom, calls=%fused_computation | custom fusion | bytes 16384 | tf_op jit(solution)/shard_map/jit(take_along_axis)/gather | solution.py:86
  274.0 6.9 scatter_custom_fusion
  280.9 2.4 reshape.171
  283.4 31.9 %all_gather.7 = f32[8,3,2]{1,2,0:T(2,128)S(1)} all-gather(f32[1,3,2]{1,2,0:T(2,128)S(1)} %copy-done.21), channel_id=1, replica_groups=mesh['tm'=8,'lev'=4] {'tm'}, dimensions={0}, use_global_device_ids=true | all-gather | bytes 216 | tf_op jit(solution)/shard_map/all_gather | solution.py:22
  315.3 0.6 fusion.23
  315.9 1.7 copy.30
  317.6 0.3 copy-done.9
  317.9 1.2 fusion.2
  319.1 425.3 %all-gather.3.cloned.1.call-done = f32[24,2,256,512]{3,2,1,0:T(8,128)} async-done(((f32[3,2,256,512]{3,2,1,0:T(8,128)}), f32[24,2,256,512]{3,2,1,0:T(8,128)}) %all-gather.3.cloned.1.call-update) | async-done | bytes 25165840 | tf_op jit(solution)/shard_map/all_gather | solution.py:22
  744.4 0.4 broadcast_in_dim.72
  744.8 20.5 %while.15 = (s32[]{:T(128)}, f32[3,2,256,512]{3,2,1,0:T(8,128)S(1)}, s32[]{:T(128)}, f32[8,3,2]{1,2,0:T(2,128)S(1)}, f32[8,3,2,256,512]{4,3,2,1,0:T(8,128)}, /*index=5*/s32[]{:T(128)}, s32[]{:T(128)}, s32[]{:T(128)}) while((s32[]{:T(128)}, f32[3,2,256,512]{3,2,1,0:T(8,128)S(1)}, s32[]{:T(128)}, f32[8,3,2]{1,2,0:T(2,128)S(1)}, ...), condition=%wide.region_10.0_spmd, body=%wide.region_9.0_spmd.sunk | while | flops 1572869 | bytes 9437439 | solution.py:30
  744.9 2.8 bitcast_add_fusion.3
  747.8 2.8 bitcast_add_fusion.3
  750.8 2.8 bitcast_add_fusion.3
  753.7 2.8 bitcast_add_fusion.3
  756.6 2.8 bitcast_add_fusion.3
  759.5 2.8 bitcast_add_fusion.3
  762.4 2.8 bitcast_add_fusion.3
  765.2 4.4 add_bitcast_fusion
  (76 shorter events, 1.6 us)
Async XLA Ops:
  7.2 114.9 %all-reduce.29.cloned.1.call-start = ((), (), s32[]{:S(2)}) async-start(), calls=%async_computation.2 | async-start | bytes 2097152 | tf_op jit(solution)/shard_map/psum | solution.py:76
  7.2 69.3 %collective-permute-start.1 = (f32[3,2,256,512]{3,2,1,0:T(8,128)}, f32[3,2,256,512]{3,2,1,0:T(8,128)S(1)}, u32[]{:S(2)}, u32[]{:S(2)}) collective-permute-start(f32[3,2,256,512]{3,2,1,0:T(8,128)} %bitcast.161), channel_id=1, source_target_pairs={{4,0},{8,4},{12,8},{16,12},{20,16},{24,20},{28,24},{5,1},{9,5},{13... | collective-permute-start | bytes 9437192 | tf_op jit(solution)/shard_map/ppermute | solution.py:17
  78.9 0.7 copy-start.19
  82.7 96.5 %all-reduce.27.cloned.1.call-start = ((), (), s32[]{:S(2)}) async-start(), calls=%async_computation.1 | async-start | bytes 2097152 | tf_op jit(solution)/shard_map/psum | solution.py:76
  122.0 1.9 copy-start.8
  125.7 1.0 copy-start.16
  130.5 1.3 copy-start.2
  130.5 6.7 copy-start
  139.7 2.5 copy-start.4
  139.7 2.5 copy-start.6
  142.2 602.2 %all-gather.3.cloned.1.call-start = ((), (), s32[]{:S(2)}) async-start(), calls=%async_computation | async-start | bytes 28311552 | tf_op jit(solution)/shard_map/all_gather | solution.py:22
  180.2 2.1 copy-start.3
  180.2 2.1 copy-start.5
  180.3 2.2 copy-start.7
  183.7 2.0 copy-start.11
  183.7 2.0 copy-start.12
  183.7 2.0 copy-start.13
  184.0 70.9 %collective-permute-start = (f32[3,2,256,512]{3,2,1,0:T(8,128)S(1)}, f32[3,2,256,512]{3,2,1,0:T(8,128)}, u32[]{:S(2)}, u32[]{:S(2)}) collective-permute-start(f32[3,2,256,512]{3,2,1,0:T(8,128)S(1)} %pad_maximum_fusion), channel_id=1, source_target_pairs={{0,4},{4,8},{8,12},{12,16},{16,20},{20,24},{24,28},{1,5},{5,9},{9,... | collective-permute-start | bytes 9437192 | tf_op jit(solution)/shard_map/ppermute | solution.py:17
  185.7 1.0 copy-start.15
  185.7 69.3 %copy-start.14 = (f32[1,3,2,256,512]{4,3,2,1,0:T(8,128)S(1)}, f32[1,3,2,256,512]{4,3,2,1,0:T(8,128)}, u32[]{:S(2)}) copy-start(f32[1,3,2,256,512]{4,3,2,1,0:T(8,128)} %param.18) | copy-start | bytes 9437188
  262.5 1.2 copy-start.10
  262.5 2.0 copy-start.17
  263.7 10.0 %copy-start.22 = (s32[2]{0:T(128)S(1)}, s32[2]{0:T(128)}, u32[]{:S(2)}) copy-start(s32[2]{0:T(128)} %constant.178) | copy-start | bytes 28
  263.7 10.1 %copy-start.23 = (s32[2]{0:T(128)S(1)}, s32[2]{0:T(128)}, u32[]{:S(2)}) copy-start(s32[2]{0:T(128)} %constant.181) | copy-start | bytes 28
  263.7 10.2 %copy-start.18 = (f32[1,2,512]{2,1,0:T(2,128)S(1)}, f32[1,2,512]{2,1,0:T(2,128)}, u32[]{:S(2)}) copy-start(f32[1,2,512]{2,1,0:T(2,128)} %param.21) | copy-start | bytes 12292
  264.6 18.8 %copy-start.21 = (f32[1,3,2]{1,2,0:T(2,128)S(1)}, f32[1,3,2]{1,2,0:T(2,128)}, u32[]{:S(2)}) copy-start(f32[1,3,2]{1,2,0:T(2,128)} %param.25) | copy-start | bytes 76
  264.6 50.7 %copy-start.20 = (f32[1,2,512]{2,1,0:T(2,128)S(1)}, f32[1,2,512]{2,1,0:T(2,128)}, u32[]{:S(2)}) copy-start(f32[1,2,512]{2,1,0:T(2,128)} %param.22) | copy-start | bytes 12292
  273.7 42.2 %copy-start.1 = (f32[3,2,256,512]{3,2,1,0:T(8,128)S(1)}, f32[3,2,256,512]{3,2,1,0:T(8,128)}, u32[]{:S(2)}) copy-start(f32[3,2,256,512]{3,2,1,0:T(8,128)} %get-tuple-element.113) | copy-start | bytes 9437188
  315.9 2.0 copy-start.9
Sparse Core Ops, SparseCore 0:
  82.8 39.1 all-reduce.28
  142.3 36.7 all-reduce.26
  262.6 481.6 all-gather.2
where the time goes:
time: 777 us; the launch traced here: 776 us
  waiting for transfers between devices  630 us (81%)
  other arithmetic  72.7 us (9%)
  blocking collectives  31.9 us (4%)
  local copies, waits for them, and re-layouts  22.7 us (3%)
  between operations  14.2 us (2%)
    all_gather x1, waiting for transfers between devices, prefix_2(): gathered = jax.tree.map(lambda a: lax.all_gather(a, axis), part)  425 us
    ppermute x2, waiting for transfers between devices, shifted(): return lax.ppermute(block, axis, route)  131 us
    psum x2, waiting for transfers between devices, shards(): column = lax.psum(jnp.sum(tangent[0], axis=0), 'lev')  74.1 us
    all_gather x1, blocking collectives, prefix_2(): gathered = jax.tree.map(lambda a: lax.all_gather(a, axis), part)  31.9 us
    add x7, other arithmetic, combine(): later[0][:, :, None, None] * earlier[1] + later[1]  19.5 us
  transfers between devices with their start and end apart: 5, of which 5 were waited for; matrix products, arithmetic and copies ran while one was open for 4% of the time, Pallas kernels for 0%

commit v1 on v0

v1 whole, which is shorter than its diff:
```python
import functools

import jax
import jax.numpy as jnp
from jax import lax
from jax.experimental import pallas as pl
from jax.experimental.pallas import tpu as pltpu
from jax.sharding import PartitionSpec as P

TIME_STEP = 0.25
ROTATION_PARAM = 0.5
COUPLING = 0.25
SPLIT = 2
MESH_ID = pl.DeviceIdType.MESH


def up(a, axis):
    n = a.shape[axis]
    tail = lax.slice_in_dim(a, 1, n, axis=axis)
    return jnp.concatenate([tail, jnp.zeros_like(lax.slice_in_dim(a, 0, 1, axis=axis))], axis=axis)


def down(a, axis):
    n = a.shape[axis]
    head = lax.slice_in_dim(a, 0, n - 1, axis=axis)
    return jnp.concatenate([jnp.zeros_like(lax.slice_in_dim(a, 0, 1, axis=axis)), head], axis=axis)


def diff_x(a):
    return up(a, a.ndim - 2) - a


def diff_y(a):
    return up(a, a.ndim - 1) - a


def back_x(a):
    return a - down(a, a.ndim - 2)


def back_y(a):
    return a - down(a, a.ndim - 1)


def step_forward(h, u, v, column, gain, depth):
    p = gain * h
    if column is not None:
        p = p + COUPLING * column[None]
    u_new = u + TIME_STEP * (ROTATION_PARAM * v - diff_x(p))
    v_new = v - TIME_STEP * (ROTATION_PARAM * u + diff_y(p))
    h_new = h - TIME_STEP * depth * (back_x(u_new) + back_y(v_new))
    return h_new, u_new, v_new


def step_back(h, u, v, gain, depth):
    w = depth * h
    u2 = u + TIME_STEP * diff_x(w)
    v2 = v + TIME_STEP * diff_y(w)
    p = TIME_STEP * (back_x(u2) + back_y(v2))
    half = TIME_STEP * ROTATION_PARAM
    return h + gain * p, u2 - half * v2, v2 + half * u2, COUPLING * jnp.sum(p, axis=0)


def second_column(pair, total_depth):
    c = pair[0]
    lap = back_x(diff_x(c)) + back_y(diff_y(c))
    return jnp.stack([c, pair[1] + (TIME_STEP * TIME_STEP * COUPLING) * total_depth * lap])


def sum_fields(fields_a, fields_b, depth_sum):
    size = lax.axis_size("lev")
    if size < 2 or size & (size - 1):
        total_depth = lax.psum(depth_sum, "lev")
        a, b = lax.psum((fields_a, fields_b), "lev")
        return second_column(a, total_depth), second_column(b, total_depth)

    def swap(x, bit):
        return lax.ppermute(x, "lev", [(i, i ^ bit) for i in range(size)])

    total_depth = depth_sum
    bit = 1
    while bit < size:
        total_depth = total_depth + swap(total_depth, bit)
        bit *= 2
    first = lax.axis_index("lev") % 2 == 0
    kept = jnp.where(first, fields_a, fields_b)
    given = jnp.where(first, fields_b, fields_a)
    kept = kept + swap(given, 1)
    bit = 2
    while bit < size:
        kept = kept + swap(kept, bit)
        bit *= 2
    kept = second_column(kept, total_depth[0])
    other = swap(kept, 1)
    return jnp.where(first, kept, other), jnp.where(first, other, kept)


def chain_kernel(
    n, chunks, per, scale, tangent, own, partner, adjoint,
    dual, chain, adjoint_in, tangent_in, carried, sent,
    t_send, t_recv, m_send, m_recv, c_send, c_recv,
):
    s = lax.axis_index("tm")
    odd = (s % 2).astype(jnp.float32)

    def remote(src, dst, send, recv, to):
        return pltpu.make_async_remote_copy(
            src_ref=src, dst_ref=dst, send_sem=send, recv_sem=recv,
            device_id={"tm": to}, device_id_type=MESH_ID,
        )

    def tangent_copy(c):
        return remote(tangent.at[c], tangent_in.at[c], t_send.at[c], t_recv.at[c], s + 1)

    def adjoint_copy(c):
        return remote(adjoint.at[c], adjoint_in.at[c], m_send.at[c], m_recv.at[c], s - 1)

    def chain_copy(c):
        return remote(sent.at[c], carried.at[c], c_send.at[c], c_recv.at[c], s + 2)

    def every(fn):
        lax.fori_loop(0, chunks, lambda c, z: (fn(c), z)[1], 0)

    barrier = pltpu.get_barrier_semaphore()
    near = ((s >= 1, s - 1), (s >= 2, s - 2), (s < n - 1, s + 1), (s < n - 2, s + 2))
    for there, who in near:
        @pl.when(there)
        def _():
            pl.semaphore_signal(barrier, inc=1, device_id={"tm": who}, device_id_type=MESH_ID)
    pl.semaphore_wait(barrier, sum(there.astype(jnp.int32) for there, _ in near))

    @pl.when(s < n - 1)
    def _():
        every(lambda c: tangent_copy(c).start())

    @pl.when(s >= 1)
    def _():
        every(lambda c: adjoint_copy(c).start())

    def one(c):
        d = scale[0, c // per]
        d_next = scale[1, c // per]

        @pl.when(s >= 1)
        def _():
            tangent_copy(c).wait_recv()

        @pl.when(s == 0)
        def _():
            tangent_in[c] = jnp.zeros(tangent_in.shape[1:], jnp.float32)

        @pl.when(s >= 2)
        def _():
            chain_copy(c).wait_recv()

        @pl.when(s < 2)
        def _():
            carried[c] = jnp.zeros(carried.shape[1:], jnp.float32)

        swap = partner[c]
        dual_here = own[c] - tangent_in[c]
        here = d * (carried[c] + odd * swap) + dual_here
        sent[c] = d_next * here + ((1.0 - odd) * swap - tangent[c])

        @pl.when(s < n - 2)
        def _():
            chain_copy(c).start()

        dual[c] = dual_here
        chain[c] = here

    every(one)

    @pl.when(s < n - 1)
    def _():
        every(lambda c: tangent_copy(c).wait_send())
        every(lambda c: adjoint_copy(c).wait_recv())

    @pl.when(s == n - 1)
    def _():
        adjoint_in[...] = jnp.zeros_like(adjoint_in)

    @pl.when(s >= 1)
    def _():
        every(lambda c: adjoint_copy(c).wait_send())

    @pl.when(s < n - 2)
    def _():
        every(lambda c: chain_copy(c).wait_send())


def run_chain(scale, tangent, own, partner, adjoint):
    n = lax.axis_size("tm")
    planes, rows, cols = tangent.shape
    per = SPLIT if rows % (8 * SPLIT) == 0 else 1
    chunks = planes * per
    shape = (chunks, rows // per, cols)
    arrays = [a.reshape(shape) for a in (tangent, own, partner, adjoint)]
    vmem = pl.BlockSpec(memory_space=pltpu.VMEM)
    out = jax.ShapeDtypeStruct(shape, jnp.float32)
    results = pl.pallas_call(
        functools.partial(chain_kernel, n, chunks, per),
        out_shape=[out] * 3,
        in_specs=[pl.BlockSpec(memory_space=pltpu.SMEM)] + [vmem] * 4,
        out_specs=[vmem] * 3,
        scratch_shapes=[pltpu.VMEM(shape, jnp.float32)] * 3
        + [pltpu.SemaphoreType.DMA((chunks,))] * 6,
        compiler_params=pltpu.CompilerParams(
            collective_id=0, has_side_effects=True, vmem_limit_bytes=56 * 1024 * 1024
        ),
        cost_estimate=pl.CostEstimate(
            flops=20 * tangent.size, bytes_accessed=40 * tangent.size, transcendentals=0
        ),
    )(scale, *arrays)
    return [r.reshape(tangent.shape) for r in results]


def shards(
    increment, multiplier, error_var, obs_cell, obs_dual, obs_var,
    level_gain, mean_depth, chain_decay,
):
    n = lax.axis_size("tm")
    state = increment[0]
    dual = multiplier[0]
    fields, levels, rows, cols = state.shape
    gain = level_gain[:, None, None]
    depth = mean_depth[:, None, None]

    own = error_var[0] * dual + state
    own, state, dual = lax.optimization_barrier((own, state, dual))
    pairs = [(i, i ^ 1) for i in range(n) if i ^ 1 < n]
    partner = lax.ppermute(own, "tm", pairs)
    decay = chain_decay[0].reshape(-1)
    decay_next = lax.ppermute(decay, "tm", [(i, i - 1) for i in range(1, n)])

    first = step_forward(state[0], state[1], state[2], None, gain, depth)
    ahead = jnp.stack([jnp.sum(state[0], axis=0), jnp.sum(first[0], axis=0)])
    b1 = step_back(dual[0], dual[1], dual[2], gain, depth)
    b2 = step_back(b1[0], b1[1], b1[2], gain, depth)
    behind = jnp.stack([b1[3], b2[3]])
    columns, bars = sum_fields(ahead, behind, jnp.sum(mean_depth, keepdims=True))

    t = step_forward(state[0], state[1], state[2], columns[0], gain, depth)
    t = step_forward(t[0], t[1], t[2], columns[1], gain, depth)
    r = step_back(b1[0] + bars[0][None], b1[1], b1[2], gain, depth)
    r = (r[0] + bars[1][None], r[1], r[2])

    flat = (fields * levels, rows, cols)
    dual_product, chain_solution, returned = run_chain(
        jnp.stack([decay, decay_next]),
        jnp.stack(t).reshape(flat), own.reshape(flat), partner.reshape(flat),
        jnp.stack(r).reshape(flat),
    )

    flat_h = state[0].reshape(levels, -1)
    picked = jnp.take_along_axis(flat_h, obs_cell[0], axis=1)
    obs_product = obs_var[0] * obs_dual[0] + picked

    def spread(cells, values):
        return jnp.zeros((flat_h.shape[1],), jnp.float32).at[cells].add(values)

    added = jax.vmap(spread)(obs_cell[0], obs_dual[0]).reshape(state[0].shape)
    state_block = (dual - returned.reshape(state.shape)).at[0].add(added)
    return (
        dual_product.reshape(increment.shape), obs_product[None],
        state_block[None], chain_solution.reshape(increment.shape),
    )


def solution(mesh):
    state = P("tm", None, "lev", None, None)
    obs = P("tm", "lev", None)
    return jax.shard_map(
        shards,
        mesh=mesh,
        in_specs=(state, state, state, obs, obs, obs, P("lev"), P("lev"), P("tm", None, "lev")),
        out_specs=(state, obs, state, state),
        check_vma=False,
    )
```

time: 777 us -> 318 us (0.41)
  waiting for transfers between devices: 630 us -> 43.2 us
  Pallas kernels: 0 us -> 163 us
  blocking collectives: 31.9 us -> 0 us
  other arithmetic: 72.7 us -> 43.3 us
  starting transfers between devices: 4.09 us -> 25.6 us
  local copies, waits for them, and re-layouts: 22.7 us -> 37.3 us
  between operations: 14.2 us -> 3.03 us
    all_gather x1 -> x0, waiting for transfers between devices: 425 us -> none  [prefix_2(): gathered = jax.tree.map(lambda a: lax.all_gather(a, axis), part)]
    pallas_call x0 -> x1, Pallas kernels: none -> 163 us  [run_chain(): pl.pallas_call(functools.partial(chain_kernel, n, chunks, per), out_shape...]
    ppermute x2 -> x7, waiting for transfers between devices: 131 us -> 43.2 us  [the longest x1 38 us: shards(): decay_next = lax.ppermute(decay, 'tm', [(i, i - 1) for i in range(1, n)])]
    psum x2 -> x0, waiting for transfers between devices: 74.1 us -> none  [shards(): column = lax.psum(jnp.sum(tangent[0], axis=0), 'lev')]
    all_gather x1 -> x0, blocking collectives: 31.9 us -> none  [prefix_2(): gathered = jax.tree.map(lambda a: lax.all_gather(a, axis), part)]
    ppermute x2 -> x7, starting transfers between devices: 3.97 us -> 25.6 us  [the longest x5 22.3 us: swap(): return lax.ppermute(x, 'lev', [(i, i ^ bit) for i in range(size)])]
    broadcast_in_dim x5 -> x0, other arithmetic: 13.6 us -> none  [the longest x4 9.25 us: dynamics_advance(): h, u, v = (state[0], state[1], state[2])]
    add x10 -> x11, other arithmetic: 24.4 us -> 14.6 us  [the longest x1 6.72 us: shards(): own = error_var[0] * dual + state]
  transfers between devices with their start and end apart: 5 -> 7, of which waited for: 5 -> 4; matrix products, arithmetic and copies ran while one was open for 4% -> 13% of each run, Pallas kernels for 0% -> 0%
where the time goes in v1:
time: 318 us; the launch traced here: 315 us
  Pallas kernels  163 us (51%)
  other arithmetic  43.3 us (14%)
  waiting for transfers between devices  43.2 us (14%)
  local copies, waits for them, and re-layouts  37.3 us (12%)
  starting transfers between devices  25.6 us (8%)
    pallas_call x1, Pallas kernels, run_chain(): pl.pallas_call(functools.partial(chain_kernel, n, chunks, per), out_shape...  163 us
    ppermute x1, waiting for transfers between devices, shards(): decay_next = lax.ppermute(decay, 'tm', [(i, i - 1) for i in range(1, n)])  38 us
    ppermute x5, starting transfers between devices, swap(): return lax.ppermute(x, 'lev', [(i, i ^ bit) for i in range(size)])  22.3 us
    unnamed x62, local copies, waits for them, and re-layouts  14.6 us
    gather x3, local copies, waits for them, and re-layouts, shards(): picked = jnp.take_along_axis(flat_h, obs_cell[0], axis=1)  12.9 us
    unnamed x5, other arithmetic  9.22 us
    slice x14, local copies, waits for them, and re-layouts, up(): tail = lax.slice_in_dim(a, 1, n, axis=axis)  6.95 us
    add x1, other arithmetic, shards(): own = error_var[0] * dual + state  6.72 us
  transfers between devices with their start and end apart: 7, of which 4 were waited for; matrix products, arithmetic and copies ran while one was open for 13% of the time, Pallas kernels for 0%

profile of v1, /device:TPU:31, one launch (start us, length us, event | category | flops | bytes accessed | tf_op | source)
XLA Modules:
  0.0 315.1 jit_solution(16366380694792436217)
XLA Ops:
  0.7 6.7 %fusion = f32[3,2,256,512]{3,2,1,0:T(8,128)} fusion(f32[1,3,2,256,512]{4,3,2,1,0:T(8,128)} %param.13, f32[1,3,2,256,512]{4,3,2,1,0:T(8,128)} %param.11, f32[1,3,2,256,512]{4,3,2,1,0:T(8,128)} %param.12), kind=kLoop, calls=%fused_computation.5 | loop fusion | flops 1572864 | bytes 12582912 | tf_op jit(solution)/shard_map/add | solution.py:229
  7.7 0.3 slice.206
  8.0 0.7 bitcast_add_fusion.2
  8.8 1.5 multiply_reduce_fusion.1
  10.3 1.3 broadcast_multiply_fusion
  11.5 1.1 slice.208
  12.6 1.3 slice.210
  13.9 0.6 copy-done
  14.8 1.1 slice.200
  15.9 1.3 slice.202
  17.2 0.6 fusion.13
  17.8 2.0 slice_bitcast_fusion
  19.8 3.1 multiply_add_fusion.6
  23.0 0.5 multiply_reduce_fusion
  23.5 0.5 copy-done.18
  24.4 0.3 copy-done.14
  24.7 0.7 bitcast_add_fusion.4
  25.4 0.6 fusion.3
  26.0 0.4 copy-done.9
  26.6 0.7 collective-permute-start.1
  27.4 2.3 collective-permute-done.1
  29.7 0.4 select_add_fusion
  30.0 0.3 collective-permute-start.2
  30.3 0.7 collective-permute-start.3
  31.0 1.0 collective-permute-done.3
  33.2 19.3 %collective-permute-start.4 = (f32[1]{0:T(128)}, f32[1]{0:T(128)}, u32[]{:S(2)}, u32[]{:S(2)}) collective-permute-start(f32[1]{0:T(128)} %add.239), channel_id=1, source_target_pairs={{0,2},{1,3},{2,0},{3,1},{4,6},{5,7},{6,4},{7,5},{8,10},{9,11},{10,... | collective-permute-start | bytes 20 | tf_op jit(solution)/shard_map/ppermute | solution.py:78
  52.5 1.9 collective-permute-done.4
  55.1 0.5 fusion.14
  56.2 0.3 fusion.8
  56.5 1.1 pad_maximum_fusion.4
  57.7 1.3 collective-permute-start.5
  58.9 0.3 collective-permute-start.6
  59.4 3.1 collective-permute-start
  62.8 7.0 %scatter_custom_fusion = f32[262144]{0:T(1024)} fusion(s32[1024]{0:T(1024)S(1)} %bitcast.173, f32[1024]{0:T(1024)S(1)} %bitcast.174, f32[]{:T(128)} %constant.75.clone.1), kind=kCustom, calls=%fused_computation.57 | custom fusion | flops 1024 | bytes 1048580
  69.8 2.4 reshape.111
  72.2 3.1 copy.17
  75.3 12.9 %gather_fusion = f32[1024]{0:T(1024)S(1)} fusion(f32[2,131072]{1,0:T(2,128)} %bitcast.143, s32[1024]{0:T(1024)S(1)} %bitcast.138), kind=kCustom, calls=%fused_computation | custom fusion | bytes 16384 | tf_op jit(solution)/shard_map/jit(take_along_axis)/gather | solution.py:256
  88.3 0.6 fusion.11
  88.9 38.0 %collective-permute-done = f32[6]{0:T(128)S(1)} collective-permute-done((f32[6]{0:T(128)S(1)}, f32[6]{0:T(128)S(1)}, u32[]{:S(2)}, u32[]{:S(2)}) %collective-permute-start) | collective-permute-done | bytes 56 | tf_op jit(solution)/shard_map/ppermute | solution.py:234
  126.9 0.5 pad_maximum_fusion.5.scale
  127.5 1.9 broadcast_select_fusion
  129.4 0.3 add_multiply_fusion
  129.9 0.3 slice.231
  130.7 0.3 slice.221
  131.1 0.8 bitcast_add_fusion.3
  131.9 0.7 multiply_add_fusion.3
  132.7 0.3 slice.226
  133.1 0.7 copy-done.4
  133.8 0.3 copy-done.6
  134.1 0.8 subtract_bitcast_fusion
  134.9 0.8 add_bitcast_fusion.1
  135.8 2.2 pad_maximum_fusion.1
  138.0 0.6 multiply_add_fusion.2
  138.7 0.5 subtract_bitcast_fusion.1
  139.2 2.2 pad_maximum_fusion
  141.4 162.6 %shard_map.120 = (f32[12,128,512]{2,1,0:T(8,128)}, f32[12,128,512]{2,1,0:T(8,128)}, f32[12,128,512]{2,1,0:T(8,128)}) custom-call(f32[2,6]{1,0:T(2,128)} %pad_maximum_fusion.5.scale, f32[12,128,512]{2,1,0:T(8,128)} %bitcast.154, f32[12,128,512]{2,1,0:T(8,128)} %bitcast.26.own, f32[12,128,512]{2,1,0:T(8,128)} %bitcast.27.partner, f32[12,128,512]{2,1,0:T(8,128)} %bitcast.153), custom_call_target="tpu_custom_call" | custom-call | flops 15728640 | bytes 31457280 | tf_op jit(solution)/shard_map/pallas_call | solution.py:201
  304.1 2.6 sub.159
  306.7 0.6 copy.21
  307.3 0.6 copy-done.12
  308.2 1.1 copy-done.16
  309.3 1.7 copy.24
  311.0 1.5 copy-done.17
  312.5 1.0 copy-done.15
  313.5 1.7 copy.25
  (76 shorter events, 3.2 us)
Async XLA Ops:
  0.6 6.7 %copy-start.1 = (f32[1,3,2,256,512]{4,3,2,1,0:T(8,128)S(1)}, f32[1,3,2,256,512]{4,3,2,1,0:T(8,128)}, u32[]{:S(2)}) copy-start(f32[1,3,2,256,512]{4,3,2,1,0:T(8,128)} %param.12) | copy-start | bytes 9437188
  0.6 6.7 %copy-start.22 = (f32[2]{0:T(128)S(1)}, f32[2]{0:T(128)}, u32[]{:S(2)}) copy-start(f32[2]{0:T(128)} %param.18) | copy-start | bytes 28
  7.4 0.7 copy-start.21
  8.8 2.8 copy-start.3
  8.8 2.8 copy-start.5
  11.5 3.2 %copy-start.8 = (f32[2,256,512]{2,1,0:T(8,128)}, f32[2,256,512]{2,1,0:T(8,128)S(1)}, u32[]{:S(2)}) copy-start(f32[2,256,512]{2,1,0:T(8,128)S(1)} %get-tuple-element.35) | copy-start | bytes 3145732
  11.5 3.0 copy-start
  23.0 1.0 copy-start.18
  23.0 1.4 copy-start.13
  23.0 1.7 copy-start.14
  25.4 1.0 copy-start.9
  26.6 3.0 collective-permute-start.1
  30.0 25.0 %collective-permute-start.2 = (f32[2,256,512]{2,1,0:T(8,128)S(1)}, f32[2,256,512]{2,1,0:T(8,128)S(1)}, u32[]{:S(2)}, u32[]{:S(2)}) collective-permute-start(f32[2,256,512]{2,1,0:T(8,128)S(1)} %select_add_fusion), channel_id=1, source_target_pairs={{0,2},{1,3},{2,0},{3,1},{4,6},{5,7},{6,4},{7,5},{8,10},{9,11},{10,... | collective-permute-start | bytes 3145736 | tf_op jit(solution)/shard_map/ppermute | solution.py:78
  30.3 1.6 collective-permute-start.3
  33.2 21.3 %collective-permute-start.4 = (f32[1]{0:T(128)}, f32[1]{0:T(128)}, u32[]{:S(2)}, u32[]{:S(2)}) collective-permute-start(f32[1]{0:T(128)} %add.239), channel_id=1, source_target_pairs={{0,2},{1,3},{2,0},{3,1},{4,6},{5,7},{6,4},{7,5},{8,10},{9,11},{10,... | collective-permute-start | bytes 20 | tf_op jit(solution)/shard_map/ppermute | solution.py:78
  55.7 0.8 copy-start.10
  56.2 3.0 copy-start.24
  56.2 6.4 %copy-start.19 = (s32[1,2,512]{2,1,0:T(2,128)S(1)}, s32[1,2,512]{2,1,0:T(2,128)}, u32[]{:S(2)}) copy-start(s32[1,2,512]{2,1,0:T(2,128)} %param.14) | copy-start | bytes 12292
  56.2 6.4 %copy-start.25 = (s32[2]{0:T(128)S(1)}, s32[2]{0:T(128)}, u32[]{:S(2)}) copy-start(s32[2]{0:T(128)} %constant.146) | copy-start | bytes 28
  56.2 6.5 %copy-start.26 = (s32[2]{0:T(128)S(1)}, s32[2]{0:T(128)}, u32[]{:S(2)}) copy-start(s32[2]{0:T(128)} %constant.149) | copy-start | bytes 28
  56.2 6.6 %copy-start.20 = (f32[1,2,512]{2,1,0:T(2,128)S(1)}, f32[1,2,512]{2,1,0:T(2,128)}, u32[]{:S(2)}) copy-start(f32[1,2,512]{2,1,0:T(2,128)} %param.15) | copy-start | bytes 12292
  56.5 1.1 copy-start.11
  57.7 69.8 %collective-permute-start.5 = (f32[2,256,512]{2,1,0:T(8,128)}, f32[2,256,512]{2,1,0:T(8,128)}, u32[]{:S(2)}, u32[]{:S(2)}) collective-permute-start(f32[2,256,512]{2,1,0:T(8,128)} %pad_maximum_fusion.4), channel_id=1, source_target_pairs={{0,1},{1,0},{2,3},{3,2},{4,5},{5,4},{6,7},{7,6},{8,9},{9,8},{10,11... | collective-permute-start | bytes 3145736 | tf_op jit(solution)/shard_map/ppermute | solution.py:78
  58.9 82.5 %collective-permute-start.6 = (f32[3,2,256,512]{3,2,1,0:T(8,128)}, f32[3,2,256,512]{3,2,1,0:T(8,128)}, u32[]{:S(2)}, u32[]{:S(2)}) collective-permute-start(f32[3,2,256,512]{3,2,1,0:T(8,128)} %fusion), channel_id=1, source_target_pairs={{0,4},{4,0},{8,12},{12,8},{16,20},{20,16},{24,28},{28,24},{1,5},{5... | collective-permute-start | bytes 9437192 | tf_op jit(solution)/shard_map/ppermute | solution.py:232
  59.4 67.6 %collective-permute-start = (f32[6]{0:T(128)S(1)}, f32[6]{0:T(128)S(1)}, u32[]{:S(2)}, u32[]{:S(2)}) collective-permute-start(f32[6]{0:T(128)S(1)} %reshape_squeeze.6), channel_id=1, source_target_pairs={{4,0},{8,4},{12,8},{16,12},{20,16},{24,20},{28,24},{5,1},{9,5},{13... | collective-permute-start | bytes 80 | tf_op jit(solution)/shard_map/ppermute | solution.py:234
  72.2 16.1 %copy-start.23 = (f32[1,2,512]{2,1,0:T(2,128)S(1)}, f32[1,2,512]{2,1,0:T(2,128)}, u32[]{:S(2)}) copy-start(f32[1,2,512]{2,1,0:T(2,128)} %param.16) | copy-start | bytes 12292
  127.5 2.0 copy-start.7
  132.6 1.2 copy-start.4
  132.6 1.5 copy-start.6
  141.4 162.6 %copy-start.2 = (f32[1,3,2,256,512]{4,3,2,1,0:T(8,128)S(1)}, f32[1,3,2,256,512]{4,3,2,1,0:T(8,128)}, u32[]{:S(2)}) copy-start(f32[1,3,2,256,512]{4,3,2,1,0:T(8,128)} %param.12) | copy-start | bytes 9437188
  306.7 1.2 copy-start.12
  307.3 2.0 copy-start.16
  309.3 3.2 %copy-start.17 = (f32[1,3,2,256,512]{4,3,2,1,0:T(8,128)}, f32[1,3,2,256,512]{4,3,2,1,0:T(8,128)S(1)}, u32[]{:S(2)}) copy-start(f32[1,3,2,256,512]{4,3,2,1,0:T(8,128)S(1)} %fusion.2) | copy-start | bytes 9437188
  309.3 4.2 %copy-start.15 = (f32[12,128,512]{2,1,0:T(8,128)S(1)}, f32[12,128,512]{2,1,0:T(8,128)}, u32[]{:S(2)}) copy-start(f32[12,128,512]{2,1,0:T(8,128)} %get-tuple-element.27) | copy-start | bytes 9437188

commit v2 on v1

--- a/solution.py
+++ b/solution.py
@@ -6,6 +6,7 @@
 from jax.experimental import pallas as pl
 from jax.experimental.pallas import tpu as pltpu
 from jax.sharding import PartitionSpec as P
+
 
 TIME_STEP = 0.25
 ROTATION_PARAM = 0.5
@@ -77,28 +78,33 @@
     def swap(x, bit):
         return lax.ppermute(x, "lev", [(i, i ^ bit) for i in range(size)])
 
-    total_depth = depth_sum
-    bit = 1
-    while bit < size:
-        total_depth = total_depth + swap(total_depth, bit)
-        bit *= 2
+    shape = fields_a.shape
+    cols = shape[-1]
+    depths = jnp.zeros((8, cols), jnp.float32) + depth_sum
+
+    def packed(fields):
+        return jnp.concatenate([fields.reshape(-1, cols), depths], axis=0)
+
     first = lax.axis_index("lev") % 2 == 0
-    kept = jnp.where(first, fields_a, fields_b)
-    given = jnp.where(first, fields_b, fields_a)
-    kept = kept + swap(given, 1)
+    kept = packed(jnp.where(first, fields_a, fields_b))
+    given = packed(jnp.where(first, fields_b, fields_a))
+    met = swap(given, 1)
+    kept = kept + met
     bit = 2
     while bit < size:
-        kept = kept + swap(kept, bit)
+        met = swap(kept, bit)
+        kept = kept + met
         bit *= 2
-    kept = second_column(kept, total_depth[0])
-    other = swap(kept, 1)
-    return jnp.where(first, kept, other), jnp.where(first, other, kept)
+    done = second_column(kept[:-8].reshape(shape), kept[-1:, :1])
+    other = swap(done, 1)
+    return jnp.where(first, done, other), jnp.where(first, other, done)
 
 
 def chain_kernel(
     n, chunks, per, scale, tangent, own, partner, adjoint,
-    dual, chain, adjoint_in, tangent_in, carried, sent,
-    t_send, t_recv, m_send, m_recv, c_send, c_recv,
+    dual, chain, adjoint_in,
+    tangent_here, own_here, partner_here, tangent_in, carried, sent, dual_here, chain_here,
+    t_send, t_recv, m_send, m_recv, c_send, c_recv, d_out, s_out, loads,
 ):
     s = lax.axis_index("tm")
     odd = (s % 2).astype(jnp.float32)
@@ -121,6 +127,17 @@
     def every(fn):
         lax.fori_loop(0, chunks, lambda c, z: (fn(c), z)[1], 0)
 
+    def dual_copy(c):
+        return pltpu.make_async_copy(dual_here.at[c], dual.at[c], d_out.at[c])
+
+    def solution_copy(c):
+        return pltpu.make_async_copy(chain_here.at[c], chain.at[c], s_out.at[c])
+
+    fetched = [
+        pltpu.make_async_copy(tangent, tangent_here, loads.at[0]),
+        pltpu.make_async_copy(own, own_here, loads.at[1]),
+        pltpu.make_async_copy(partner, partner_here, loads.at[2]),
+    ]
     barrier = pltpu.get_barrier_semaphore()
     near = ((s >= 1, s - 1), (s >= 2, s - 2), (s < n - 1, s + 1), (s < n - 2, s + 2))
     for there, who in near:
@@ -137,6 +154,11 @@
     def _():
         every(lambda c: adjoint_copy(c).start())
 
+    for copy in fetched:
+        copy.start()
+    for copy in fetched:
+        copy.wait()
+
     def one(c):
         d = scale[0, c // per]
         d_next = scale[1, c // per]
@@ -157,17 +179,19 @@
         def _():
             carried[c] = jnp.zeros(carried.shape[1:], jnp.float32)
 
-        swap = partner[c]
-        dual_here = own[c] - tangent_in[c]
-        here = d * (carried[c] + odd * swap) + dual_here
-        sent[c] = d_next * here + ((1.0 - odd) * swap - tangent[c])
+        swap = partner_here[c]
+        product_here = own_here[c] - tangent_in[c]
+        here = d * (carried[c] + odd * swap) + product_here
+        sent[c] = d_next * here + ((1.0 - odd) * swap - tangent_here[c])
 
         @pl.when(s < n - 2)
         def _():
             chain_copy(c).start()
 
-        dual[c] = dual_here
-        chain[c] = here
+        dual_here[c] = product_here
+        chain_here[c] = here
+        dual_copy(c).start()
+        solution_copy(c).start()
 
     every(one)
 
@@ -176,9 +200,8 @@
         every(lambda c: tangent_copy(c).wait_send())
         every(lambda c: adjoint_copy(c).wait_recv())
 
-    @pl.when(s == n - 1)
-    def _():
-        adjoint_in[...] = jnp.zeros_like(adjoint_in)
+    every(lambda c: dual_copy(c).wait())
+    every(lambda c: solution_copy(c).wait())
 
     @pl.when(s >= 1)
     def _():
@@ -196,15 +219,16 @@
     chunks = planes * per
     shape = (chunks, rows // per, cols)
     arrays = [a.reshape(shape) for a in (tangent, own, partner, adjoint)]
-    vmem = pl.BlockSpec(memory_space=pltpu.VMEM)
+    place = pl.BlockSpec(memory_space=pl.ANY)
     out = jax.ShapeDtypeStruct(shape, jnp.float32)
     results = pl.pallas_call(
         functools.partial(chain_kernel, n, chunks, per),
         out_shape=[out] * 3,
-        in_specs=[pl.BlockSpec(memory_space=pltpu.SMEM)] + [vmem] * 4,
-        out_specs=[vmem] * 3,
-        scratch_shapes=[pltpu.VMEM(shape, jnp.float32)] * 3
-        + [pltpu.SemaphoreType.DMA((chunks,))] * 6,
+        in_specs=[pl.BlockSpec(memory_space=pltpu.SMEM)] + [place] * 4,
+        out_specs=[place] * 3,
+        scratch_shapes=[pltpu.VMEM(shape, jnp.float32)] * 8
+        + [pltpu.SemaphoreType.DMA((chunks,))] * 8
+        + [pltpu.SemaphoreType.DMA((3,))],
         compiler_params=pltpu.CompilerParams(
             collective_id=0, has_side_effects=True, vmem_limit_bytes=56 * 1024 * 1024
         ),
@@ -215,7 +239,7 @@
     return [r.reshape(tangent.shape) for r in results]
 
 
-def shards(
+def product(
     increment, multiplier, error_var, obs_cell, obs_dual, obs_var,
     level_gain, mean_depth, chain_decay,
 ):
@@ -252,7 +276,7 @@
         jnp.stack(r).reshape(flat),
     )
 
-    flat_h = state[0].reshape(levels, -1)
+    flat_h = increment[0, 0].reshape(levels, -1)
     picked = jnp.take_along_axis(flat_h, obs_cell[0], axis=1)
     obs_product = obs_var[0] * obs_dual[0] + picked
 
@@ -260,7 +284,8 @@
         return jnp.zeros((flat_h.shape[1],), jnp.float32).at[cells].add(values)
 
     added = jax.vmap(spread)(obs_cell[0], obs_dual[0]).reshape(state[0].shape)
-    state_block = (dual - returned.reshape(state.shape)).at[0].add(added)
+    returned = jnp.where(lax.axis_index("tm") < n - 1, returned.reshape(state.shape), 0.0)
+    state_block = (dual - returned).at[0].add(added)
     return (
         dual_product.reshape(increment.shape), obs_product[None],
         state_block[None], chain_solution.reshape(increment.shape),
@@ -271,7 +296,7 @@
     state = P("tm", None, "lev", None, None)
     obs = P("tm", "lev", None)
     return jax.shard_map(
-        shards,
+        product,
         mesh=mesh,
         in_specs=(state, state, state, obs, obs, obs, P("lev"), P("lev"), P("tm", None, "lev")),
         out_specs=(state, obs, state, state),

time: 318 us -> 287 us (0.903)
  starting transfers between devices: 25.6 us -> 5.56 us
  waiting for transfers between devices: 43.2 us -> 33.9 us
  Pallas kernels: 163 us -> 156 us
  other arithmetic: 43.3 us -> 48.7 us
    ppermute x2, waiting for transfers between devices: 38 us -> 10.4 us  [the longest x1 10.4 us: product(): decay_next = lax.ppermute(decay, 'tm', [(i, i - 1) for i in range(1, n)])]
    ppermute x5 -> x3, starting transfers between devices: 22.3 us -> 2.2 us  [swap(): return lax.ppermute(x, 'lev', [(i, i ^ bit) for i in range(size)])]
    ppermute x5 -> x3, waiting for transfers between devices: 5.18 us -> 23.4 us  [swap(): return lax.ppermute(x, 'lev', [(i, i ^ bit) for i in range(size)])]
    pallas_call x1, Pallas kernels: 163 us -> 156 us  [run_chain(): pl.pallas_call(functools.partial(chain_kernel, n, chunks, per), out_shape...]
    reduce_sum x2 -> x3, other arithmetic: 1.19 us -> 4.49 us  [the longest x2 3.89 us: product(): ahead = jnp.stack([jnp.sum(state[0], axis=0), jnp.sum(first[0], axis=0)])]
    unnamed x5 -> x4, other arithmetic: 9.22 us -> 7.09 us
    unnamed x62 -> x63, local copies, waits for them, and re-layouts: 14.6 us -> 13.8 us
  transfers between devices with their start and end apart: 7 -> 5, of which waited for: 4 -> 3; matrix products, arithmetic and copies ran while one was open for 13% -> 15% of each run, Pallas kernels for 0% -> 0%
where the time goes in v2:
time: 287 us; the launch traced here: 283 us
  Pallas kernels  156 us (54%)
  other arithmetic  48.7 us (17%)
  local copies, waits for them, and re-layouts  36.6 us (13%)
  waiting for transfers between devices  33.9 us (12%)
  starting transfers between devices  5.56 us (2%)
    pallas_call x1, Pallas kernels, run_chain(): pl.pallas_call(functools.partial(chain_kernel, n, chunks, per), out_shape...  156 us
    ppermute x3, waiting for transfers between devices, swap(): return lax.ppermute(x, 'lev', [(i, i ^ bit) for i in range(size)])  23.4 us
    gather x3, local copies, waits for them, and re-layouts, product(): picked = jnp.take_along_axis(flat_h, obs_cell[0], axis=1)  13.9 us
    unnamed x63, local copies, waits for them, and re-layouts  13.8 us
    ppermute x1, waiting for transfers between devices, product(): decay_next = lax.ppermute(decay, 'tm', [(i, i - 1) for i in range(1, n)])  10.4 us
    unnamed x4, other arithmetic  7.09 us
    add x1, other arithmetic, product(): own = error_var[0] * dual + state  6.72 us
  transfers between devices with their start and end apart: 5, of which 3 were waited for; matrix products, arithmetic and copies ran while one was open for 15% of the time, Pallas kernels for 0%

profile of v2, /device:TPU:31, one launch (start us, length us, event | category | flops | bytes accessed | tf_op | source)
XLA Modules:
  0.0 282.7 jit_solution(8281796751865187275)
XLA Ops:
  0.7 6.7 %fusion = f32[3,2,256,512]{3,2,1,0:T(8,128)} fusion(f32[1,3,2,256,512]{4,3,2,1,0:T(8,128)} %param.13, f32[1,3,2,256,512]{4,3,2,1,0:T(8,128)} %param.11, f32[1,3,2,256,512]{4,3,2,1,0:T(8,128)} %param.12), kind=kLoop, calls=%fused_computation.5 | loop fusion | flops 1572864 | bytes 12582912 | tf_op jit(solution)/shard_map/add | solution.py:253
  7.7 0.3 slice.215
  8.1 1.2 copy-done.1
  9.3 2.3 bitcast_add_fusion.4
  11.7 0.3 slice.219
  12.0 0.6 bitcast_add_fusion.2
  12.7 1.5 multiply_reduce_fusion.1
  14.2 1.3 broadcast_multiply_fusion
  15.4 1.2 slice.221
  16.8 1.3 slice.223
  18.1 0.6 fusion.12
  18.7 0.9 slice_reduce_fusion
  19.5 3.1 %multiply_add_fusion.6 = (f32[2,256,512]{2,1,0:T(8,128)S(1)}, f32[2,256,512]{2,1,0:T(8,128)S(1)}) fusion(f32[2,256,512]{2,1,0:T(8,128)} %copy-done.8, f32[2,255,512]{2,1,0:T(8,128)} %slice.221, f32[2,256,512]{2,1,0:T(8,128)} %copy-done.3, f32[2,256,512]{2,1,0:T(8,128)} %copy-done.5, f32[2,256,511]{2,1,0:T(8,128)} %slice.223), kind=kLoop, calls=%fused_computation.41 | loop fusion | flops 2621440 | bytes 7333888 | tf_op jit(solution)/shard_map/add | solution.py:58
  22.7 0.5 multiply_reduce_fusion
  23.2 0.8 multiply_bitcast_fusion
  24.1 0.8 multiply_bitcast_fusion.1
  24.9 3.0 %fusion.3 = f32[256,512]{1,0:T(8,128)S(1)} fusion(f32[2,256,512]{2,1,0:T(8,128)} %get-tuple-element.40, f32[2,256,511]{2,1,0:T(8,128)} %bitcast.148, f32[2,256,512]{2,1,0:T(8,128)} %get-tuple-element.39, f32[2,255,512]{2,1,0:T(8,128)} %bitcast.147, f32[3,2,256,512]{3,2,1,0:T(8,128)S(1)} %bitcast.123, f32[2]{0:T(128)S(1)} %get-tuple-element.63), kind=kLoop, calls=%fused_computation.27 | loop fusion | flops 1441792 | bytes 5761032 | tf_op jit(solution)/shard_map/reduce_sum | solution.py:261
  28.0 0.3 fusion.5
  28.3 0.7 concatenate.105
  29.0 0.7 collective-permute-start.1
  29.8 2.3 collective-permute-done.1
  32.1 1.8 pad_add_fusion
  34.1 0.3 collective-permute-start.4
  34.6 3.1 %collective-permute-start = (f32[6]{0:T(128)S(1)}, f32[6]{0:T(128)S(1)}, u32[]{:S(2)}, u32[]{:S(2)}) collective-permute-start(f32[6]{0:T(128)S(1)} %reshape_squeeze.6), channel_id=1, source_target_pairs={{4,0},{8,4},{12,8},{16,12},{20,16},{24,20},{28,24},{5,1},{9,5},{13... | collective-permute-start | bytes 80 | tf_op jit(solution)/shard_map/ppermute | solution.py:258
  37.8 21.1 %collective-permute-done.2 = f32[520,512]{1,0:T(8,128)} collective-permute-done((f32[520,512]{1,0:T(8,128)}, f32[520,512]{1,0:T(8,128)}, u32[]{:S(2)}, u32[]{:S(2)}) %collective-permute-start.2) | collective-permute-done | bytes 1064992 | tf_op jit(solution)/shard_map/ppermute | solution.py:79
  58.9 1.8 add.239
  60.9 0.5 slice.227
  62.5 0.3 fusion.8
  62.8 1.1 pad_maximum_fusion.4
  63.9 1.2 collective-permute-start.3
  65.4 6.9 %scatter_custom_fusion = f32[262144]{0:T(1024)} fusion(s32[1024]{0:T(1024)S(1)} %bitcast.160, f32[1024]{0:T(1024)S(1)} %bitcast.161, f32[]{:T(128)} %constant.78.clone.1), kind=kCustom, calls=%fused_computation.57 | custom fusion | flops 1024 | bytes 1048580
  72.3 2.4 reshape.128
  74.8 1.8 copy.17
  76.6 13.9 %gather_fusion = f32[1024]{0:T(1024)S(1)} fusion(f32[2,131072]{1,0:T(2,128)} %bitcast.134, s32[1024]{0:T(1024)S(1)} %bitcast.127), kind=kCustom, calls=%fused_computation | custom fusion | bytes 16384 | tf_op jit(solution)/shard_map/jit(take_along_axis)/gather | solution.py:280
  90.5 0.6 fusion.11
  91.1 10.4 %collective-permute-done = f32[6]{0:T(128)S(1)} collective-permute-done((f32[6]{0:T(128)S(1)}, f32[6]{0:T(128)S(1)}, u32[]{:S(2)}, u32[]{:S(2)}) %collective-permute-start) | collective-permute-done | bytes 56 | tf_op jit(solution)/shard_map/ppermute | solution.py:258
  101.5 0.5 pad_maximum_fusion.5.scale
  102.0 1.9 broadcast_select_fusion.1
  104.0 0.3 add_multiply_fusion
  104.5 0.3 slice.245
  104.9 0.2 broadcast_add_fusion
  105.3 0.3 slice.235
  105.7 0.8 bitcast_add_fusion.3
  106.4 0.7 multiply_add_fusion.3
  107.3 0.3 slice.240
  107.6 0.7 copy-done.4
  108.4 0.3 copy-done.6
  108.7 0.8 subtract_bitcast_fusion
  109.5 0.8 add_bitcast_fusion.1
  110.3 2.2 pad_maximum_fusion.1
  112.6 0.6 multiply_add_fusion.2
  113.2 0.5 subtract_bitcast_fusion.1
  113.8 2.2 pad_maximum_fusion
  116.0 155.9 %shard_map.120 = (f32[12,128,512]{2,1,0:T(8,128)}, f32[12,128,512]{2,1,0:T(8,128)}, f32[12,128,512]{2,1,0:T(8,128)}) custom-call(f32[2,6]{1,0:T(2,128)} %pad_maximum_fusion.5.scale, f32[12,128,512]{2,1,0:T(8,128)} %bitcast.143, f32[12,128,512]{2,1,0:T(8,128)} %bitcast.25.own, f32[12,128,512]{2,1,0:T(8,128)} %bitcast.26.partner, f32[12,128,512]{2,1,0:T(8,128)} %bitcast.142), custom_call_target="tpu_custom_call" | custom-call | flops 15728640 | bytes 31457280 | tf_op jit(solution)/shard_map/pallas_call | solution.py:224
  271.9 0.4 broadcast_select_fusion
  272.3 1.5 copy-done.2
  273.8 0.7 sub.159
  274.6 0.3 copy.21
  274.9 0.9 copy-done.11
  276.0 0.9 copy-done.13
  276.8 1.7 copy.24
  278.5 1.5 copy-done.14
  280.0 1.0 copy-done.12
  281.0 1.7 copy.25
  (75 shorter events, 2.7 us)
Async XLA Ops:
  0.6 6.7 %copy-start = (f32[1,3,2,256,512]{4,3,2,1,0:T(8,128)S(1)}, f32[1,3,2,256,512]{4,3,2,1,0:T(8,128)}, u32[]{:S(2)}) copy-start(f32[1,3,2,256,512]{4,3,2,1,0:T(8,128)} %param.11) | copy-start | bytes 9437188
  0.6 6.7 %copy-start.21 = (f32[2]{0:T(128)S(1)}, f32[2]{0:T(128)}, u32[]{:S(2)}) copy-start(f32[2]{0:T(128)} %param.17) | copy-start | bytes 28
  7.4 1.9 copy-start.1
  7.4 1.9 copy-start.22
  12.7 2.8 copy-start.3
  12.7 2.8 copy-start.5
  15.4 1.3 copy-start.8
  22.7 1.4 copy-start.18
  24.9 3.1 %copy-start.15 = (f32[256,512]{1,0:T(8,128)S(1)}, f32[256,512]{1,0:T(8,128)}, u32[]{:S(2)}) copy-start(f32[256,512]{1,0:T(8,128)} %slice_reduce_fusion) | copy-start | bytes 1572868
  24.9 3.1 %copy-start.16 = (f32[1,256,512]{2,1,0:T(8,128)S(1)}, f32[1,256,512]{2,1,0:T(8,128)}, u32[]{:S(2)}) copy-start(f32[1,256,512]{2,1,0:T(8,128)} %multiply_bitcast_fusion) | copy-start | bytes 1572868
  24.9 3.1 %copy-start.17 = (f32[1,256,512]{2,1,0:T(8,128)S(1)}, f32[1,256,512]{2,1,0:T(8,128)}, u32[]{:S(2)}) copy-start(f32[1,256,512]{2,1,0:T(8,128)} %multiply_bitcast_fusion.1) | copy-start | bytes 1572868
  28.3 6.1 %copy-start.24 = (f32[1,3,2]{1,2,0:T(2,128)S(1)}, f32[1,3,2]{1,2,0:T(2,128)}, u32[]{:S(2)}) copy-start(f32[1,3,2]{1,2,0:T(2,128)} %param.19) | copy-start | bytes 76
  28.3 9.5 %copy-start.19 = (s32[1,2,512]{2,1,0:T(2,128)S(1)}, s32[1,2,512]{2,1,0:T(2,128)}, u32[]{:S(2)}) copy-start(s32[1,2,512]{2,1,0:T(2,128)} %param.14) | copy-start | bytes 12292
  29.0 3.1 %collective-permute-start.1 = (f32[520,512]{1,0:T(8,128)S(1)}, f32[520,512]{1,0:T(8,128)S(1)}, u32[]{:S(2)}, u32[]{:S(2)}) collective-permute-start(f32[520,512]{1,0:T(8,128)S(1)} %concatenate.105), channel_id=1, source_target_pairs={{0,1},{1,0},{2,3},{3,2},{4,5},{5,4},{6,7},{7,6},{8,9},{9,8},{10,11... | collective-permute-start | bytes 3194888 | tf_op jit(solution)/shard_map/ppermute | solution.py:79
  33.9 25.0 %collective-permute-start.2 = (f32[520,512]{1,0:T(8,128)}, f32[520,512]{1,0:T(8,128)}, u32[]{:S(2)}, u32[]{:S(2)}) collective-permute-start(f32[520,512]{1,0:T(8,128)} %pad_add_fusion), channel_id=1, source_target_pairs={{0,2},{1,3},{2,0},{3,1},{4,6},{5,7},{6,4},{7,5},{8,10},{9,11},{10,... | collective-permute-start | bytes 3194888 | tf_op jit(solution)/shard_map/ppermute | solution.py:79
  34.1 81.9 %collective-permute-start.4 = (f32[3,2,256,512]{3,2,1,0:T(8,128)}, f32[3,2,256,512]{3,2,1,0:T(8,128)}, u32[]{:S(2)}, u32[]{:S(2)}) collective-permute-start(f32[3,2,256,512]{3,2,1,0:T(8,128)} %fusion), channel_id=1, source_target_pairs={{0,4},{4,0},{8,12},{12,8},{16,20},{20,16},{24,28},{28,24},{1,5},{5... | collective-permute-start | bytes 9437192 | tf_op jit(solution)/shard_map/ppermute | solution.py:256
  34.6 66.9 %collective-permute-start = (f32[6]{0:T(128)S(1)}, f32[6]{0:T(128)S(1)}, u32[]{:S(2)}, u32[]{:S(2)}) collective-permute-start(f32[6]{0:T(128)S(1)} %reshape_squeeze.6), channel_id=1, source_target_pairs={{4,0},{8,4},{12,8},{16,12},{20,16},{24,20},{28,24},{5,1},{9,5},{13... | collective-permute-start | bytes 80 | tf_op jit(solution)/shard_map/ppermute | solution.py:258
  61.7 1.1 copy-start.9
  61.7 3.5 %copy-start.25 = (s32[2]{0:T(128)S(1)}, s32[2]{0:T(128)}, u32[]{:S(2)}) copy-start(s32[2]{0:T(128)} %constant.156) | copy-start | bytes 28
  61.7 3.6 %copy-start.26 = (s32[2]{0:T(128)S(1)}, s32[2]{0:T(128)}, u32[]{:S(2)}) copy-start(s32[2]{0:T(128)} %constant.159) | copy-start | bytes 28
  61.7 3.7 %copy-start.20 = (f32[1,2,512]{2,1,0:T(2,128)S(1)}, f32[1,2,512]{2,1,0:T(2,128)}, u32[]{:S(2)}) copy-start(f32[1,2,512]{2,1,0:T(2,128)} %param.15) | copy-start | bytes 12292
  62.8 1.1 copy-start.10
  63.9 38.1 %collective-permute-start.3 = (f32[2,256,512]{2,1,0:T(8,128)}, f32[2,256,512]{2,1,0:T(8,128)}, u32[]{:S(2)}, u32[]{:S(2)}) collective-permute-start(f32[2,256,512]{2,1,0:T(8,128)} %pad_maximum_fusion.4), channel_id=1, source_target_pairs={{0,1},{1,0},{2,3},{3,2},{4,5},{5,4},{6,7},{7,6},{8,9},{9,8},{10,11... | collective-permute-start | bytes 3145736 | tf_op jit(solution)/shard_map/ppermute | solution.py:79
  74.8 15.7 %copy-start.23 = (f32[1,2,512]{2,1,0:T(2,128)S(1)}, f32[1,2,512]{2,1,0:T(2,128)}, u32[]{:S(2)}) copy-start(f32[1,2,512]{2,1,0:T(2,128)} %param.16) | copy-start | bytes 12292
  102.0 2.0 copy-start.7
  107.1 1.2 copy-start.4
  107.1 1.5 copy-start.6
  271.9 1.9 copy-start.2
  274.6 1.2 copy-start.11
  274.9 2.0 copy-start.13
  276.8 3.2 %copy-start.14 = (f32[1,3,2,256,512]{4,3,2,1,0:T(8,128)}, f32[1,3,2,256,512]{4,3,2,1,0:T(8,128)S(1)}, u32[]{:S(2)}) copy-start(f32[1,3,2,256,512]{4,3,2,1,0:T(8,128)S(1)} %fusion.2) | copy-start | bytes 9437188
  276.8 4.2 %copy-start.12 = (f32[12,128,512]{2,1,0:T(8,128)S(1)}, f32[12,128,512]{2,1,0:T(8,128)}, u32[]{:S(2)}) copy-start(f32[12,128,512]{2,1,0:T(8,128)} %get-tuple-element.27) | copy-start | bytes 9437188

commit v3 on v2

--- a/solution.py
+++ b/solution.py
@@ -68,12 +68,12 @@
     return jnp.stack([c, pair[1] + (TIME_STEP * TIME_STEP * COUPLING) * total_depth * lap])
 
 
-def sum_fields(fields_a, fields_b, depth_sum):
+def sum_fields(fields_a, fields_b, depth_sum, beside):
     size = lax.axis_size("lev")
     if size < 2 or size & (size - 1):
         total_depth = lax.psum(depth_sum, "lev")
         a, b = lax.psum((fields_a, fields_b), "lev")
-        return second_column(a, total_depth), second_column(b, total_depth)
+        return second_column(a, total_depth), second_column(b, total_depth), beside
 
     def swap(x, bit):
         return lax.ppermute(x, "lev", [(i, i ^ bit) for i in range(size)])
@@ -93,11 +93,12 @@
     bit = 2
     while bit < size:
         met = swap(kept, bit)
+        met, beside = lax.optimization_barrier((met, beside))
         kept = kept + met
         bit *= 2
     done = second_column(kept[:-8].reshape(shape), kept[-1:, :1])
     other = swap(done, 1)
-    return jnp.where(first, done, other), jnp.where(first, other, done)
+    return jnp.where(first, done, other), jnp.where(first, other, done), beside
 
 
 def chain_kernel(
@@ -257,12 +258,22 @@
     decay = chain_decay[0].reshape(-1)
     decay_next = lax.ppermute(decay, "tm", [(i, i - 1) for i in range(1, n)])
 
+    flat_h = increment[0, 0].reshape(levels, -1)
+    picked = jnp.take_along_axis(flat_h, obs_cell[0], axis=1)
+    obs_product = obs_var[0] * obs_dual[0] + picked
+
+    def spread(cells, values):
+        return jnp.zeros((flat_h.shape[1],), jnp.float32).at[cells].add(values)
+
+    added = jax.vmap(spread)(obs_cell[0], obs_dual[0]).reshape(state[0].shape)
     first = step_forward(state[0], state[1], state[2], None, gain, depth)
     ahead = jnp.stack([jnp.sum(state[0], axis=0), jnp.sum(first[0], axis=0)])
     b1 = step_back(dual[0], dual[1], dual[2], gain, depth)
     b2 = step_back(b1[0], b1[1], b1[2], gain, depth)
     behind = jnp.stack([b1[3], b2[3]])
-    columns, bars = sum_fields(ahead, behind, jnp.sum(mean_depth, keepdims=True))
+    columns, bars, added = sum_fields(
+        ahead, behind, jnp.sum(mean_depth, keepdims=True), added
+    )
 
     t = step_forward(state[0], state[1], state[2], columns[0], gain, depth)
     t = step_forward(t[0], t[1], t[2], columns[1], gain, depth)
@@ -276,14 +287,6 @@
         jnp.stack(r).reshape(flat),
     )
 
-    flat_h = increment[0, 0].reshape(levels, -1)
-    picked = jnp.take_along_axis(flat_h, obs_cell[0], axis=1)
-    obs_product = obs_var[0] * obs_dual[0] + picked
-
-    def spread(cells, values):
-        return jnp.zeros((flat_h.shape[1],), jnp.float32).at[cells].add(values)
-
-    added = jax.vmap(spread)(obs_cell[0], obs_dual[0]).reshape(state[0].shape)
     returned = jnp.where(lax.axis_index("tm") < n - 1, returned.reshape(state.shape), 0.0)
     state_block = (dual - returned).at[0].add(added)
     return (

time: 287 us -> 304 us (1.059)
  waiting for transfers between devices: 33.9 us -> 55.1 us
    ppermute x1, waiting for transfers between devices: 0.01 us -> 37.6 us  [product(): partner = lax.ppermute(own, 'tm', pairs)]
    ppermute x1, waiting for transfers between devices: 10.4 us -> 0.01 us  [product(): decay_next = lax.ppermute(decay, 'tm', [(i, i - 1) for i in range(1, n)])]
    ppermute x3, waiting for transfers between devices: 23.4 us -> 17.5 us  [swap(): return lax.ppermute(x, 'lev', [(i, i ^ bit) for i in range(size)])]
    unnamed x63 -> x61, local copies, waits for them, and re-layouts: 13.8 us -> 14.5 us
    unnamed x4 -> x5, other arithmetic: 7.09 us -> 7.1 us
    gather x3 -> x2, local copies, waits for them, and re-layouts: 13.9 us -> 13.9 us  [product(): picked = jnp.take_along_axis(flat_h, obs_cell[0], axis=1)]
  transfers between devices with their start and end apart: 5 -> 5, of which waited for: 3 -> 3; matrix products, arithmetic and copies ran while one was open for 15% -> 13% of each run, Pallas kernels for 0% -> 0%
where the time goes in v3:
time: 304 us; the launch traced here: 301 us
  Pallas kernels  155 us (51%)
  waiting for transfers between devices  55.1 us (18%)
  other arithmetic  46.4 us (15%)
  local copies, waits for them, and re-layouts  37.4 us (12%)
  starting transfers between devices  5.69 us (2%)
    pallas_call x1, Pallas kernels, run_chain(): pl.pallas_call(functools.partial(chain_kernel, n, chunks, per), out_shape...  155 us
    ppermute x1, waiting for transfers between devices, product(): partner = lax.ppermute(own, 'tm', pairs)  37.6 us
    ppermute x3, waiting for transfers between devices, swap(): return lax.ppermute(x, 'lev', [(i, i ^ bit) for i in range(size)])  17.5 us
    unnamed x61, local copies, waits for them, and re-layouts  14.5 us
    gather x2, local copies, waits for them, and re-layouts, product(): picked = jnp.take_along_axis(flat_h, obs_cell[0], axis=1)  13.9 us
    unnamed x5, other arithmetic  7.1 us
    add x1, other arithmetic, product(): own = error_var[0] * dual + state  6.72 us
  transfers between devices with their start and end apart: 5, of which 3 were waited for; matrix products, arithmetic and copies ran while one was open for 13% of the time, Pallas kernels for 0%

profile of v3, /device:TPU:31, one launch (start us, length us, event | category | flops | bytes accessed | tf_op | source)
XLA Modules:
  0.0 301.1 jit_solution(5393693751495627334)
XLA Ops:
  0.6 0.7 broadcast_multiply_fusion.1
  1.3 6.7 %fusion = f32[3,2,256,512]{3,2,1,0:T(8,128)} fusion(f32[1,3,2,256,512]{4,3,2,1,0:T(8,128)} %param.13, f32[1,3,2,256,512]{4,3,2,1,0:T(8,128)} %param.11, f32[1,3,2,256,512]{4,3,2,1,0:T(8,128)} %param.12), kind=kLoop, calls=%fused_computation.5 | loop fusion | flops 1572864 | bytes 12582912 | tf_op jit(solution)/shard_map/add | solution.py:254
  8.0 0.9 slice_reduce_fusion
  9.1 0.3 slice.215
  9.6 0.6 fusion.12
  10.2 0.6 copy-done.1
  10.8 2.3 bitcast_add_fusion.4
  13.1 0.3 slice.219
  13.6 0.6 bitcast_add_fusion.2
  14.2 1.5 multiply_reduce_fusion.1
  15.7 1.3 broadcast_multiply_fusion
  17.0 1.3 slice.223
  18.4 1.1 slice.221
  19.4 1.1 multiply_bitcast_fusion.1
  20.5 3.1 %multiply_add_fusion.6 = (f32[2,256,512]{2,1,0:T(8,128)S(1)}, f32[2,256,512]{2,1,0:T(8,128)S(1)}) fusion(f32[2,256,512]{2,1,0:T(8,128)} %copy-done.8, f32[2,255,512]{2,1,0:T(8,128)} %slice.221, f32[2,256,512]{2,1,0:T(8,128)} %copy-done.3, f32[2,256,512]{2,1,0:T(8,128)} %copy-done.5, f32[2,256,511]{2,1,0:T(8,128)} %slice.223), kind=kLoop, calls=%fused_computation.41 | loop fusion | flops 2621440 | bytes 7333888 | tf_op jit(solution)/shard_map/add | solution.py:58
  23.7 0.5 multiply_reduce_fusion
  24.3 0.6 copy-done.9
  24.9 0.3 copy-done.10
  25.2 0.6 fusion.3
  26.1 0.7 concatenate.105
  26.9 0.7 collective-permute-start.1
  27.6 2.3 collective-permute-done.1
  29.9 1.8 pad_add_fusion
  32.2 6.9 %scatter_custom_fusion = f32[262144]{0:T(1024)} fusion(s32[1024]{0:T(1024)S(1)} %bitcast.164, f32[1024]{0:T(1024)S(1)} %bitcast.163, f32[]{:T(128)} %constant.78.clone.1), kind=kCustom, calls=%fused_computation.57 | custom fusion | flops 1024 | bytes 1048580
  39.1 2.4 reshape.130
  41.6 15.2 %collective-permute-done.2 = f32[520,512]{1,0:T(8,128)} collective-permute-done((f32[520,512]{1,0:T(8,128)}, f32[520,512]{1,0:T(8,128)}, u32[]{:S(2)}, u32[]{:S(2)}) %collective-permute-start.2) | collective-permute-done | bytes 1064992 | tf_op jit(solution)/shard_map/ppermute | solution.py:79
  56.8 1.8 add.241
  58.5 0.5 slice.227
  60.5 0.5 copy-done.11
  61.0 1.0 pad_maximum_fusion.4
  62.1 1.2 collective-permute-start.3
  63.5 2.3 collective-permute-start
  65.8 1.2 collective-permute-start.4
  67.1 1.8 copy.19
  68.9 13.9 %gather_fusion = f32[1024]{0:T(1024)S(1)} fusion(f32[2,131072]{1,0:T(2,128)} %bitcast.136, s32[1024]{0:T(1024)S(1)} %bitcast.129), kind=kCustom, calls=%fused_computation | custom fusion | bytes 16384 | tf_op jit(solution)/shard_map/jit(take_along_axis)/gather | solution.py:262
  82.8 0.6 fusion.11
  83.4 0.5 pad_maximum_fusion.5.scale
  84.0 1.9 broadcast_select_fusion.1
  86.0 0.3 add_multiply_fusion
  86.3 0.3 slice.245
  87.1 0.3 slice.235
  87.6 0.8 bitcast_add_fusion.3
  88.4 0.7 multiply_add_fusion.3
  89.1 0.3 slice.240
  89.6 0.7 copy-done.4
  90.3 0.3 copy-done.6
  90.6 0.8 subtract_bitcast_fusion
  91.5 0.8 add_bitcast_fusion.1
  92.3 2.2 pad_maximum_fusion.1
  94.5 0.6 multiply_add_fusion.2
  95.2 0.5 subtract_bitcast_fusion.1
  95.7 2.2 pad_maximum_fusion
  98.0 37.6 %collective-permute-done.4 = f32[3,2,256,512]{3,2,1,0:T(8,128)} collective-permute-done((f32[3,2,256,512]{3,2,1,0:T(8,128)}, f32[3,2,256,512]{3,2,1,0:T(8,128)}, u32[]{:S(2)}, u32[]{:S(2)}) %collective-permute-start.4) | collective-permute-done | bytes 3145760 | tf_op jit(solution)/shard_map/ppermute | solution.py:257
  135.6 154.8 %shard_map.120 = (f32[12,128,512]{2,1,0:T(8,128)}, f32[12,128,512]{2,1,0:T(8,128)}, f32[12,128,512]{2,1,0:T(8,128)}) custom-call(f32[2,6]{1,0:T(2,128)} %pad_maximum_fusion.5.scale, f32[12,128,512]{2,1,0:T(8,128)} %bitcast.145, f32[12,128,512]{2,1,0:T(8,128)} %bitcast.147, f32[12,128,512]{2,1,0:T(8,128)} %bitcast.27.partner, f32[12,128,512]{2,1,0:T(8,128)} %bitcast.144), custom_call_target="tpu_custom_call" | custom-call | flops 15728640 | bytes 31457280 | tf_op jit(solution)/shard_map/pallas_call | solution.py:225
  290.4 0.4 broadcast_select_fusion
  290.7 1.5 copy-done.2
  292.2 0.7 sub.159
  293.0 0.3 copy.21
  293.3 0.9 copy-done.13
  294.4 0.9 copy-done.15
  295.3 1.7 copy.24
  297.0 1.5 copy-done.16
  298.5 1.0 copy-done.14
  299.5 1.7 copy.25
  (73 shorter events, 3.4 us)
Async XLA Ops:
  1.3 6.7 %copy-start = (f32[1,3,2,256,512]{4,3,2,1,0:T(8,128)S(1)}, f32[1,3,2,256,512]{4,3,2,1,0:T(8,128)}, u32[]{:S(2)}) copy-start(f32[1,3,2,256,512]{4,3,2,1,0:T(8,128)} %param.11) | copy-start | bytes 9437188
  1.3 7.6 %copy-start.20 = (f32[2]{0:T(128)S(1)}, f32[2]{0:T(128)}, u32[]{:S(2)}) copy-start(f32[2]{0:T(128)} %param.17) | copy-start | bytes 28
  8.9 0.7 copy-start.21
  8.9 1.9 copy-start.1
  14.2 2.8 copy-start.3
  14.2 2.8 copy-start.5
  17.0 1.3 copy-start.8
  23.7 1.2 copy-start.9
  23.7 1.5 copy-start.10
  24.3 1.5 copy-start.17
  26.1 5.9 %copy-start.19 = (f32[1,2,512]{2,1,0:T(2,128)S(1)}, f32[1,2,512]{2,1,0:T(2,128)}, u32[]{:S(2)}) copy-start(f32[1,2,512]{2,1,0:T(2,128)} %param.15) | copy-start | bytes 12292
  26.1 5.9 %copy-start.18 = (s32[1,2,512]{2,1,0:T(2,128)S(1)}, s32[1,2,512]{2,1,0:T(2,128)}, u32[]{:S(2)}) copy-start(s32[1,2,512]{2,1,0:T(2,128)} %param.14) | copy-start | bytes 12292
  26.1 5.9 %copy-start.24 = (s32[2]{0:T(128)S(1)}, s32[2]{0:T(128)}, u32[]{:S(2)}) copy-start(s32[2]{0:T(128)} %constant.156) | copy-start | bytes 28
  26.1 6.0 %copy-start.25 = (s32[2]{0:T(128)S(1)}, s32[2]{0:T(128)}, u32[]{:S(2)}) copy-start(s32[2]{0:T(128)} %constant.159) | copy-start | bytes 28
  26.9 3.1 %collective-permute-start.1 = (f32[520,512]{1,0:T(8,128)S(1)}, f32[520,512]{1,0:T(8,128)S(1)}, u32[]{:S(2)}, u32[]{:S(2)}) collective-permute-start(f32[520,512]{1,0:T(8,128)S(1)} %concatenate.105), channel_id=1, source_target_pairs={{0,1},{1,0},{2,3},{3,2},{4,5},{5,4},{6,7},{7,6},{8,9},{9,8},{10,11... | collective-permute-start | bytes 3194888 | tf_op jit(solution)/shard_map/ppermute | solution.py:79
  31.8 25.0 %collective-permute-start.2 = (f32[520,512]{1,0:T(8,128)}, f32[520,512]{1,0:T(8,128)}, u32[]{:S(2)}, u32[]{:S(2)}) collective-permute-start(f32[520,512]{1,0:T(8,128)} %pad_add_fusion), channel_id=1, source_target_pairs={{0,2},{1,3},{2,0},{3,1},{4,6},{5,7},{6,4},{7,5},{8,10},{9,11},{10,... | collective-permute-start | bytes 3194888 | tf_op jit(solution)/shard_map/ppermute | solution.py:79
  60.2 0.9 copy-start.11
  60.2 3.1 %copy-start.23 = (f32[1,3,2]{1,2,0:T(2,128)S(1)}, f32[1,3,2]{1,2,0:T(2,128)}, u32[]{:S(2)}) copy-start(f32[1,3,2]{1,2,0:T(2,128)} %param.19) | copy-start | bytes 76
  60.5 1.6 copy-start.12
  62.1 21.9 %collective-permute-start.3 = (f32[2,256,512]{2,1,0:T(8,128)}, f32[2,256,512]{2,1,0:T(8,128)}, u32[]{:S(2)}, u32[]{:S(2)}) collective-permute-start(f32[2,256,512]{2,1,0:T(8,128)} %pad_maximum_fusion.4), channel_id=1, source_target_pairs={{0,1},{1,0},{2,3},{3,2},{4,5},{5,4},{6,7},{7,6},{8,9},{9,8},{10,11... | collective-permute-start | bytes 3145736 | tf_op jit(solution)/shard_map/ppermute | solution.py:79
  63.5 20.0 %collective-permute-start = (f32[6]{0:T(128)S(1)}, f32[6]{0:T(128)S(1)}, u32[]{:S(2)}, u32[]{:S(2)}) collective-permute-start(f32[6]{0:T(128)S(1)} %reshape_squeeze.6), channel_id=1, source_target_pairs={{4,0},{8,4},{12,8},{16,12},{20,16},{24,20},{28,24},{5,1},{9,5},{13... | collective-permute-start | bytes 80 | tf_op jit(solution)/shard_map/ppermute | solution.py:259
  65.8 69.8 %collective-permute-start.4 = (f32[3,2,256,512]{3,2,1,0:T(8,128)}, f32[3,2,256,512]{3,2,1,0:T(8,128)}, u32[]{:S(2)}, u32[]{:S(2)}) collective-permute-start(f32[3,2,256,512]{3,2,1,0:T(8,128)} %fusion), channel_id=1, source_target_pairs={{0,4},{4,0},{8,12},{12,8},{16,20},{20,16},{24,28},{28,24},{1,5},{5... | collective-permute-start | bytes 9437192 | tf_op jit(solution)/shard_map/ppermute | solution.py:257
  67.1 15.7 %copy-start.22 = (f32[1,2,512]{2,1,0:T(2,128)S(1)}, f32[1,2,512]{2,1,0:T(2,128)}, u32[]{:S(2)}) copy-start(f32[1,2,512]{2,1,0:T(2,128)} %param.16) | copy-start | bytes 12292
  84.0 2.0 copy-start.7
  89.1 1.2 copy-start.4
  89.1 1.5 copy-start.6
  290.3 1.9 copy-start.2
  293.0 1.2 copy-start.13
  293.3 2.0 copy-start.15
  295.3 3.2 %copy-start.16 = (f32[1,3,2,256,512]{4,3,2,1,0:T(8,128)}, f32[1,3,2,256,512]{4,3,2,1,0:T(8,128)S(1)}, u32[]{:S(2)}) copy-start(f32[1,3,2,256,512]{4,3,2,1,0:T(8,128)S(1)} %fusion.2) | copy-start | bytes 9437188
  295.3 4.2 %copy-start.14 = (f32[12,128,512]{2,1,0:T(8,128)S(1)}, f32[12,128,512]{2,1,0:T(8,128)}, u32[]{:S(2)}) copy-start(f32[12,128,512]{2,1,0:T(8,128)} %get-tuple-element.31) | copy-start | bytes 9437188
